TPU v7x, 32 devices: a whole 2x2x4 slice. The times are simulated.
32 devices in a mesh: scan: 2 (over y), ang: 4 (over z), row: 4 (over x, core).
Axes of the slice: x: 2, y: 2, z: 4, core: 2. Of those that a mesh axis runs over, the one named last changes fastest.
Arguments:
- projections: bfloat16 [8, 32, 2560], P(('scan', 'ang'), 'row'), parts along dimension 0, may hold values from 0 to 2
- flats: float32 [64, 2560], P(('scan', 'row')), parts along dimension 0, may hold values from 1 to 3
- block_start: int32 [4, 4], replicated, may hold values from 0 to 2528
- bp_weights: bfloat16 [4, 32, 1024], P(None, None, 'ang'), may hold values from -0.5 to 0.5
Outputs:
- recon: float32 [64, 1024], P(('scan', 'row'), 'ang'), parts along dimension 0
There are 2 independent parts, one for each index of `scan`. A program takes and returns all parts, laid end to end along the dimension named above; an argument that names none is the same for every part. Nothing has to cross between parts.
Inputs may be any that keep to these rules, and one draw needn't show every extreme that they name: block_start[a, r] is the first of the 32 detector columns that pixel region r reads at angle a.
All inputs are finite; a program needn't handle non-finite values.
Results may differ from a plain program's by a relative error of at most 0.009.
Values may be sent and summed in bfloat16 or wider, within the bound.
A program may use at most 64 MiB of HBM per device.

v0:
```python
import jax
import jax.numpy as jnp
from jax import lax
from jax.sharding import PartitionSpec as P

HALO = 4


paganin_beta = 8.0
ramp_gain = 320.0
highest = lax.Precision.HIGHEST


def with_halo(x, sides, width):
    for axis, dim in sides:
        peers, length = (lax.axis_size(axis), x.shape[dim])
        up = [(i, (i + 1) % peers) for i in range(peers - 1)]
        down = [(j, i) for i, j in up]
        last = lax.slice_in_dim(x, length - width, length, axis=dim)
        initial = lax.slice_in_dim(x, 0, width, axis=dim)
        before = lax.ppermute(last, axis, up)
        after = lax.ppermute(initial, axis, down)
        x = jnp.concatenate([before, x, after], axis=dim)
    return x


def contract(form, left, right):
    return jnp.einsum(form, left, right, precision=highest)


def circle_table(count):
    index = jnp.arange(count, dtype=jnp.int32)
    phase = index[:, None] * index[None, :] % count
    angle = 2.0 * jnp.pi / count * phase.astype(jnp.float32)
    return (jnp.cos(angle), jnp.sin(angle))


def twiddle_table(blocks, width):
    first = jnp.arange(blocks, dtype=jnp.int32)
    second = jnp.arange(128, dtype=jnp.int32)
    phase = first[:, None] * second[None, :] % width
    angle = 2.0 * jnp.pi / width * phase.astype(jnp.float32)
    return (jnp.cos(angle), jnp.sin(angle))


def columns_forward(values, tables):
    outer_cos, outer_sin, turn_cos, turn_sin, inner_cos, inner_sin = tables
    first_re = contract("...ab,ak->...kb", values, outer_cos)
    first_im = -contract("...ab,ak->...kb", values, outer_sin)
    turned_re = first_re * turn_cos + first_im * turn_sin
    turned_im = first_im * turn_cos - first_re * turn_sin
    spec_re = contract("...kb,bm->...km", turned_re, inner_cos) + contract(
        "...kb,bm->...km", turned_im, inner_sin
    )
    spec_im = contract("...kb,bm->...km", turned_im, inner_cos) - contract(
        "...kb,bm->...km", turned_re, inner_sin
    )
    return (spec_re, spec_im)


def columns_inverse(spec_re, spec_im, tables):
    outer_cos, outer_sin, turn_cos, turn_sin, inner_cos, inner_sin = tables
    back_re = contract("...km,bm->...kb", spec_re, inner_cos) - contract(
        "...km,bm->...kb", spec_im, inner_sin
    )
    back_im = contract("...km,bm->...kb", spec_im, inner_cos) + contract(
        "...km,bm->...kb", spec_re, inner_sin
    )
    untwist_re = back_re * turn_cos - back_im * turn_sin
    untwist_im = back_im * turn_cos + back_re * turn_sin
    values = contract("...kb,ak->...ab", untwist_re, outer_cos) - contract(
        "...kb,ak->...ab", untwist_im, outer_sin
    )
    return values / (outer_cos.shape[0] * 128)


def body(projections, flats, block_start, bp_weights):
    angles_dev, rows_dev, width = projections.shape
    blocks_count = width // 128
    tile_rows = rows_dev + 2 * HALO
    cb_width = bp_weights.shape[1]
    outer_cos, outer_sin = circle_table(blocks_count)
    turn_cos, turn_sin = twiddle_table(blocks_count, width)
    inner_cos, inner_sin = circle_table(128)
    tables = (outer_cos, outer_sin, turn_cos, turn_sin, inner_cos, inner_sin)
    row_cos, row_sin = circle_table(tile_rows)
    freq_index = (
        jnp.arange(blocks_count, dtype=jnp.int32)[:, None]
        + blocks_count * jnp.arange(128, dtype=jnp.int32)[None, :]
    )
    col_freq = freq_index.astype(jnp.float32)
    row_freq = jnp.arange(tile_rows, dtype=jnp.float32)
    lam = (4.0 * jnp.sin(jnp.pi * row_freq / tile_rows) ** 2)[:, None, None] + (
        4.0 * jnp.sin(jnp.pi * col_freq / width) ** 2
    )[None, :, :]
    filt = 1.0 / (1.0 + paganin_beta * lam)
    folded = jnp.minimum(col_freq, width - col_freq)
    ramp = ramp_gain * (folded / width) * (0.5 + 0.5 * jnp.cos(2.0 * jnp.pi * folded / width))
    contrast = 1.0 - projections.astype(jnp.float32) / flats[None, :, :]
    shaped = contrast.reshape(angles_dev, rows_dev, blocks_count, 128)
    widened = with_halo(shaped.astype(jnp.bfloat16), (("row", 1),), HALO).astype(shaped.dtype)
    spec_re, spec_im = columns_forward(widened, tables)
    rows_re = contract("tk,atbm->akbm", row_cos, spec_re) + contract(
        "tk,atbm->akbm", row_sin, spec_im
    )
    rows_im = contract("tk,atbm->akbm", row_cos, spec_im) - contract(
        "tk,atbm->akbm", row_sin, spec_re
    )
    rows_re = rows_re * filt
    rows_im = rows_im * filt
    inner_rcos = row_cos[HALO : HALO + rows_dev]
    inner_rsin = row_sin[HALO : HALO + rows_dev]
    kept_re = (
        contract("tk,akbm->atbm", inner_rcos, rows_re)
        - contract("tk,akbm->atbm", inner_rsin, rows_im)
    ) / tile_rows
    kept_im = (
        contract("tk,akbm->atbm", inner_rcos, rows_im)
        + contract("tk,akbm->atbm", inner_rsin, rows_re)
    ) / tile_rows
    filtered = columns_inverse(kept_re * ramp, kept_im * ramp, tables)
    sinogram = filtered.reshape(angles_dev, rows_dev, width).astype(jnp.bfloat16)
    region = lax.axis_index("ang")

    def cut_block(sheet, begin):
        return lax.dynamic_slice(sheet, (0, begin), (rows_dev, cb_width))

    my_column = lax.dynamic_index_in_dim(block_start, region, 1, keepdims=False)
    blocks = jax.vmap(cut_block)(lax.all_gather(sinogram, "ang", axis=0, tiled=True), my_column)
    return jnp.einsum("arc,acp->rp", blocks, bp_weights, preferred_element_type=jnp.float32)


def solution(mesh):
    placed = (P(("scan", "ang"), "row", None), P(("scan", "row"), None), P(), P(None, None, "ang"))
    return jax.shard_map(
        body, mesh=mesh, in_specs=placed, out_specs=P(("scan", "row"), "ang"), check_vma=False
    )
```

profile of v0, /device:TPU:0, one launch (start us, length us, event | category | flops | bytes accessed | tf_op | source)
XLA Modules:
  0.0 33.9 jit_solution(8301812078791457497)
XLA Ops:
  0.0 0.9 %fusion.61 = bf16[1,8,20,128]{3,1,2,0:T(8,128)(2,1)S(1)} fusion(f32[8,2560]{1,0:T(8,128)} %param.5, bf16[1,8,2560]{2,1,0:T(8,128)(2,1)} %param.4), kind=kLoop, calls=%fused_computation.82 | loop fusion | flops 81920 | bytes 163840 | tf_op jit(solution)/shard_map/convert_element_type | solution.py:101
  1.0 2.4 %collective-permute-start = (bf16[1,4,20,128]{3,2,1,0:T(8,128)(2,1)S(1)}, bf16[1,4,20,128]{3,2,1,0:T(8,128)(2,1)S(1)}, u32[]{:S(2)}, u32[]{:S(2)}) collective-permute-start(bf16[1,4,20,128]{3,2,1,0:T(8,128)(2,1)S(1)} %get-tuple-element.5), channel_id=1, source_target_pairs={{0,1},{1,2},{2,3},{4,5},{5,6},{6,7},{8,9},{9,10},{10,11},{12,13},{... | collective-permute-start | bytes 61448 | tf_op jit(solution)/shard_map/ppermute | solution.py:21
  3.4 1.3 %collective-permute-start.1 = (bf16[1,4,20,128]{3,2,1,0:T(8,128)(2,1)S(1)}, bf16[1,4,20,128]{3,2,1,0:T(8,128)(2,1)S(1)}, u32[]{:S(2)}, u32[]{:S(2)}) collective-permute-start(bf16[1,4,20,128]{3,2,1,0:T(8,128)(2,1)S(1)} %get-tuple-element.6), channel_id=1, source_target_pairs={{1,0},{2,1},{3,2},{5,4},{6,5},{7,6},{9,8},{10,9},{11,10},{13,12},{... | collective-permute-start | bytes 61448 | tf_op jit(solution)/shard_map/ppermute | solution.py:22
  4.7 0.1 fusion.83
  4.8 0.1 fusion.118
  4.9 0.1 multiply_multiply_fusion
  5.1 0.9 %fusion.128 = s32[4]{0:T(128)S(1)} fusion(s32[4,4]{1,0:T(4,128)} %param.6, s32[]{:T(128)S(6)} %select_n.92), kind=kLoop, calls=%fused_computation.143 | loop fusion | flops 32 | bytes 36 | tf_op jit(solution)/shard_map/vmap()/gather | solution.py:126
  5.9 2.6 %collective-permute-done.1 = bf16[1,4,20,128]{3,2,1,0:T(8,128)(2,1)S(1)} collective-permute-done((bf16[1,4,20,128]{3,2,1,0:T(8,128)(2,1)S(1)}, bf16[1,4,20,128]{3,2,1,0:T(8,128)(2,1)S(1)}, u32[]{:S(2)}, u32[]{:S(2)}) %collective-permute-start.1) | collective-permute-done | bytes 20512 | tf_op jit(solution)/shard_map/ppermute | solution.py:22
  8.6 0.4 %fusion = f32[20,1,16,128]{3,0,2,1:T(8,128)S(1)} fusion(bf16[1,4,20,128]{3,2,1,0:T(8,128)(2,1)S(1)} %collective-permute-done.1, bf16[1,8,20,128]{3,2,1,0:T(8,128)(2,1)S(1)} %copy.40, bf16[1,4,20,128]{3,2,1,0:T(8,128)(2,1)S(1)} %collective-permute-done), kind=kOutput, calls=%fused_computation.4 | convolution fusion | flops 10120720 | bytes 245760 | tf_op jit(solution)/shard_map/...ab,ak->...kb/dot_general | solution.py:28
  8.9 0.4 %convolution_bitcast_fusion = f32[20,1,16,128]{3,0,2,1:T(8,128)S(1)} fusion(bf16[1,4,20,128]{3,2,1,0:T(8,128)(2,1)S(1)} %collective-permute-done.1, bf16[1,8,20,128]{3,2,1,0:T(8,128)(2,1)S(1)} %copy.40, bf16[1,4,20,128]{3,2,1,0:T(8,128)(2,1)S(1)} %collective-permute-done), kind=kOutput, calls=%fused_computation.5 | convolution fusion | flops 10079760 | bytes 245760 | tf_op jit(solution)/shard_map/...ab,ak->...kb/dot_general | solution.py:28
  9.3 0.6 %fusion.17 = f32[16,20,128]{2,1,0:T(8,128)S(1)} fusion(f32[20,1,16,128]{3,0,2,1:T(8,128)S(1)} %fusion, f32[20,1,16,128]{3,0,2,1:T(8,128)S(1)} %convolution_bitcast_fusion, f32[20,128]{1,0:T(8,128)S(1)} %get-tuple-element.9, f32[20,128]{1,0:T(8,128)S(1)} %get-tuple-element.10), kind=kOutput, calls=%fused_computation.30 | convolution fusion | flops 63266816 | bytes 512000 | tf_op jit(solution)/shard_map/...kb,bm->...km/dot_general | solution.py:28
  9.9 0.6 %fusion.19 = f32[16,20,128]{2,1,0:T(8,128)S(1)} fusion(f32[20,1,16,128]{3,0,2,1:T(8,128)S(1)} %convolution_bitcast_fusion, f32[20,1,16,128]{3,0,2,1:T(8,128)S(1)} %fusion, f32[20,128]{1,0:T(8,128)S(1)} %get-tuple-element.9, f32[20,128]{1,0:T(8,128)S(1)} %get-tuple-element.10), kind=kOutput, calls=%fused_computation.32 | convolution fusion | flops 63266816 | bytes 512000 | tf_op jit(solution)/shard_map/...kb,bm->...km/dot_general | solution.py:28
  10.4 0.6 %convolution_add_fusion = f32[16,20,128]{2,1,0:T(8,128)S(1)} fusion(f32[16,20,128]{2,1,0:T(8,128)S(1)} %fusion.17, f32[20,1,16,128]{3,0,2,1:T(8,128)S(1)} %convolution_bitcast_fusion, f32[20,1,16,128]{3,0,2,1:T(8,128)S(1)} %fusion, f32[20,128]{1,0:T(8,128)S(1)} %get-tuple-element.9, f32[20,128]{1,0:T(8,128)S(1)} %get-tuple-element.10), kind=kOutput, calls=%fused_computation.2 | convolution fusion | flops 63307776 | bytes 675840 | tf_op jit(solution)/shard_map/...kb,bm->...km/dot_general | solution.py:28
  11.0 0.4 %fusion.26 = f32[20,128,16]{1,2,0:T(8,128)S(1)} fusion(f32[16,20,128]{2,1,0:T(8,128)S(1)} %convolution_add_fusion), kind=kOutput, calls=%fused_computation.42 | convolution fusion | flops 7867904 | bytes 327680 | tf_op jit(solution)/shard_map/tk,atbm->akbm/dot_general | solution.py:28
  11.4 0.6 %convolution_subtract_fusion = f32[16,20,128]{2,1,0:T(8,128)S(1)} fusion(f32[16,20,128]{2,1,0:T(8,128)S(1)} %fusion.19, f32[20,1,16,128]{3,0,2,1:T(8,128)S(1)} %fusion, f32[20,1,16,128]{3,0,2,1:T(8,128)S(1)} %convolution_bitcast_fusion, f32[20,128]{1,0:T(8,128)S(1)} %get-tuple-element.9, f32[20,128]{1,0:T(8,128)S(1)} %get-tuple-element.10), kind=kOutput, calls=%fused_computation.1 | convolution fusion | flops 63307776 | bytes 675840 | tf_op jit(solution)/shard_map/...kb,bm->...km/dot_general | solution.py:28
  12.0 0.4 %fusion.22 = f32[20,128,16]{1,2,0:T(8,128)S(1)} fusion(f32[16,20,128]{2,1,0:T(8,128)S(1)} %convolution_subtract_fusion), kind=kOutput, calls=%fused_computation.38 | convolution fusion | flops 7867904 | bytes 327680 | tf_op jit(solution)/shard_map/tk,atbm->akbm/dot_general | solution.py:28
  12.4 0.4 %fusion.4 = f32[16,20,128]{2,0,1:T(8,128)S(1)} fusion(f32[20,128,16]{1,2,0:T(8,128)S(1)} %fusion.26, f32[16,20,128]{2,1,0:T(8,128)S(1)} %convolution_subtract_fusion, f32[20,128]{1,0:T(8,128)S(1)} %get-tuple-element.8, f32[16]{0:T(128)S(1)} %multiply_multiply_fusion.2), kind=kOutput, calls=%fused_computation.11 | convolution fusion | flops 8113664 | bytes 501824 | tf_op jit(solution)/shard_map/tk,atbm->akbm/dot_general | solution.py:28
  12.8 0.4 %fusion.6 = f32[16,20,128]{2,0,1:T(8,128)S(1)} fusion(f32[20,128,16]{1,2,0:T(8,128)S(1)} %fusion.22, f32[16,20,128]{2,1,0:T(8,128)S(1)} %convolution_add_fusion, f32[20,128]{1,0:T(8,128)S(1)} %get-tuple-element.8, f32[16]{0:T(128)S(1)} %multiply_multiply_fusion.2), kind=kOutput, calls=%fused_computation.13 | convolution fusion | flops 8113664 | bytes 501824 | tf_op jit(solution)/shard_map/tk,atbm->akbm/dot_general | solution.py:28
  13.2 0.2 fusion.124
  13.4 0.2 fusion.123
  13.7 0.2 fusion.12
  13.9 0.5 %fusion.32 = f32[8,20,128]{2,1,0:T(8,128)S(1)} fusion(f32[8,20,128]{2,0,1:T(8,128)S(1)} %fusion.12), kind=kOutput, calls=%fused_computation.48 | convolution fusion | flops 31686656 | bytes 163840 | tf_op jit(solution)/shard_map/...km,bm->...kb/dot_general | solution.py:28
  14.4 0.2 fusion.14
  14.6 0.5 %fusion.28 = f32[8,20,128]{2,1,0:T(8,128)S(1)} fusion(f32[8,20,128]{2,0,1:T(8,128)S(1)} %fusion.14), kind=kOutput, calls=%fused_computation.44 | convolution fusion | flops 31686656 | bytes 163840 | tf_op jit(solution)/shard_map/...km,bm->...kb/dot_general | solution.py:28
  15.1 0.5 %convolution_subtract_fusion.3 = f32[8,20,128]{2,1,0:T(8,128)S(1)} fusion(f32[8,20,128]{2,1,0:T(8,128)S(1)} %fusion.32, f32[8,20,128]{2,0,1:T(8,128)S(1)} %fusion.14), kind=kOutput, calls=%fused_computation.17 | convolution fusion | flops 31707136 | bytes 245760 | tf_op jit(solution)/shard_map/...km,bm->...kb/dot_general | solution.py:28
  15.6 0.5 %convolution_add_fusion.2 = f32[8,20,128]{2,1,0:T(8,128)S(1)} fusion(f32[8,20,128]{2,1,0:T(8,128)S(1)} %fusion.28, f32[8,20,128]{2,0,1:T(8,128)S(1)} %fusion.12), kind=kOutput, calls=%fused_computation.16 | convolution fusion | flops 31707136 | bytes 245760 | tf_op jit(solution)/shard_map/...km,bm->...kb/dot_general | solution.py:28
  16.1 0.3 fusion.37
  16.5 0.3 fusion.15
  16.8 14.0 %all_gather.3 = bf16[4,8,2560]{2,1,0:T(8,128)(2,1)S(1)} all-gather(bf16[1,8,2560]{2,1,0:T(8,128)(2,1)S(1)} %convert_element_type.129), channel_id=1, replica_groups=mesh['scan'=2,'ang'=4,'row'=4] {'ang'}, dimensions={0}, use_global_device_ids=true | all-gather | bytes 204800 | tf_op jit(solution)/shard_map/all_gather | solution.py:129
  30.8 1.5 %copy.57 = bf16[4,8,2560]{1,0,2:T(4,128)(2,1)S(1)} copy(bf16[4,8,2560]{2,1,0:T(8,128)(2,1)S(1)} %all_gather.3) | data formatting | bytes 327680 | tf_op jit(solution)/shard_map/all_gather | solution.py:129
  32.3 0.7 %gather_fusion = bf16[4,8,32]{1,0,2:T(4,128)(2,1)S(1)} fusion(bf16[4,8,2560]{1,0,2:T(4,128)(2,1)S(1)} %copy.57, s32[4]{0:T(128)S(1)} %fusion.128), kind=kCustom, calls=%fused_computation | custom fusion | bytes 4144 | tf_op jit(solution)/shard_map/vmap()/gather | solution.py:126
  33.1 0.8 %convolution_bitcast_fusion.1 = f32[8,256]{1,0:T(8,128)} fusion(bf16[4,32,256]{2,1,0:T(8,128)(2,1)S(1)} %copy-done, bf16[4,8,32]{1,0,2:T(4,128)(2,1)S(1)} %gather_fusion), kind=kOutput, calls=%fused_computation.28 | convolution fusion | flops 524288 | bytes 75776 | tf_op jit(solution)/shard_map/arc,acp->rp/dot_general | solution.py:130
  (9 shorter events, 0.2 us)
Async XLA Ops:
  0.0 33.1 %copy-start = (bf16[4,32,256]{2,1,0:T(8,128)(2,1)S(1)}, bf16[4,32,256]{2,1,0:T(8,128)(2,1)}, u32[]{:S(2)}) copy-start(bf16[4,32,256]{2,1,0:T(8,128)(2,1)} %param.7) | copy-start | bytes 196612
  1.0 5.0 %collective-permute-start = (bf16[1,4,20,128]{3,2,1,0:T(8,128)(2,1)S(1)}, bf16[1,4,20,128]{3,2,1,0:T(8,128)(2,1)S(1)}, u32[]{:S(2)}, u32[]{:S(2)}) collective-permute-start(bf16[1,4,20,128]{3,2,1,0:T(8,128)(2,1)S(1)} %get-tuple-element.5), channel_id=1, source_target_pairs={{0,1},{1,2},{2,3},{4,5},{5,6},{6,7},{8,9},{9,10},{10,11},{12,13},{... | collective-permute-start | bytes 61448 | tf_op jit(solution)/shard_map/ppermute | solution.py:21
  3.4 5.2 %collective-permute-start.1 = (bf16[1,4,20,128]{3,2,1,0:T(8,128)(2,1)S(1)}, bf16[1,4,20,128]{3,2,1,0:T(8,128)(2,1)S(1)}, u32[]{:S(2)}, u32[]{:S(2)}) collective-permute-start(bf16[1,4,20,128]{3,2,1,0:T(8,128)(2,1)S(1)} %get-tuple-element.6), channel_id=1, source_target_pairs={{1,0},{2,1},{3,2},{5,4},{6,5},{7,6},{9,8},{10,9},{11,10},{13,12},{... | collective-permute-start | bytes 61448 | tf_op jit(solution)/shard_map/ppermute | solution.py:22
where the time goes:
time: 34.1 us; the launch traced here: 33.9 us
  blocking collectives  14 us (41%)
  matrix products  8.87 us (26%)
  starting transfers between devices  3.69 us (11%)
  waiting for transfers between devices  2.63 us (8%)
  local copies, waits for them, and re-layouts  2.31 us (7%)
  other arithmetic  2.17 us (6%)
    all_gather x1, blocking collectives, body(): lax.all_gather(sinogram, 'ang', axis=0, tiled=True)  14 us
    dot_general x20, matrix products, contract(): return jnp.einsum(form, left, right, precision=highest)  8.09 us
    ppermute x1, waiting for transfers between devices, with_halo(): after = lax.ppermute(initial, axis, down)  2.63 us
    ppermute x1, starting transfers between devices, with_halo(): before = lax.ppermute(last, axis, up)  2.4 us
    all_gather x1, local copies, waits for them, and re-layouts, body(): lax.all_gather(sinogram, 'ang', axis=0, tiled=True)  1.5 us
    ppermute x1, starting transfers between devices, with_halo(): after = lax.ppermute(initial, axis, down)  1.29 us
    convert_element_type x1, other arithmetic, body(): shaped.astype(jnp.bfloat16)  0.94 us
    gather x1, other arithmetic, cut_block(): return lax.dynamic_slice(sheet, (0, begin), (rows_dev, cb_width))  0.87 us
  transfers between devices with their start and end apart: 2, of which 1 were waited for; matrix products, arithmetic and copies ran while one was open for 4% of the time, Pallas kernels for 0%

commit v1 on v0

v1 whole, which is shorter than its diff:
```python
import functools

import jax
import jax.numpy as jnp
import numpy as np
from jax import lax
from jax.experimental import pallas as pl
from jax.experimental.pallas import tpu as pltpu
from jax.sharding import PartitionSpec as P

HALO = 4
LANES = 128
CHUNK = 512
paganin_beta = 8.0
ramp_gain = 320.0


def filter_table(tile_rows, width, cb_width):
    u = np.arange(tile_rows, dtype=np.float64)
    v = np.arange(width, dtype=np.float64)
    lam = (4.0 * np.sin(np.pi * u / tile_rows) ** 2)[:, None] + (4.0 * np.sin(np.pi * v / width) ** 2)[None, :]
    folded = np.minimum(v, width - v)
    ramp = ramp_gain * (folded / width) * (0.5 + 0.5 * np.cos(2.0 * np.pi * folded / width))
    taps = np.real(np.fft.ifft2(ramp[None, :] / (1.0 + paganin_beta * lam)))
    lags = tile_rows // 2 + 1
    place = (np.arange(cb_width)[:, None] - np.arange(width)[None, :]) % width
    table = taps[:lags][:, place].reshape(lags * cb_width, width)
    chunks = width // CHUNK
    return table.reshape(lags * cb_width, chunks, CHUNK).transpose(1, 0, 2)


def kernel(regions, tiles, starts, proj, flats, table, weights, out,
           starts_s, proj_v, flats_v, table_v, weights_v, xs, ys, sbuf, rbuf, out_v,
           load_sem, table_sem, out_sem, send_sem, recv_sem):
    rows, width = flats.shape
    blocks = width // LANES
    chunks = table.shape[0]
    angles, cb, _ = weights.shape
    per = LANES // cb
    half = rows // 2
    me = lax.axis_index("ang")
    row = lax.axis_index("row")

    def peer(step, delta):
        return {"ang": lax.rem(me + step, regions), "row": lax.rem(row + delta + tiles, tiles)}

    links = [(step, delta) for step in range(regions) for delta in (-1, 0, 1) if (step, delta) != (0, 0)]
    barrier = pltpu.get_barrier_semaphore()
    for step, delta in links:
        pl.semaphore_signal(barrier, inc=1, device_id=peer(step, delta), device_id_type=pl.DeviceIdType.MESH)

    loads = [pltpu.make_async_copy(proj.at[0], proj_v, load_sem.at[0]),
             pltpu.make_async_copy(flats, flats_v, load_sem.at[1]),
             pltpu.make_async_copy(starts, starts_s, load_sem.at[3])]
    late = [pltpu.make_async_copy(table.at[k], table_v.at[k], table_sem.at[k]) for k in range(chunks)]
    weight_load = pltpu.make_async_copy(weights, weights_v, load_sem.at[2])
    for copy in loads + late + [weight_load]:
        copy.start()
    for copy in loads:
        copy.wait()

    pieces = [slice(b * LANES, (b + 1) * LANES) for b in range(blocks)]
    contrast = [1.0 - proj_v[:, p].astype(jnp.float32) / flats_v[:, p] for p in pieces]
    mean = jnp.sum(sum(contrast), axis=1, keepdims=True) / width
    for b, x in enumerate(contrast):
        xs[b] = x - mean
        xs[b + blocks] = x - mean

    lane = lax.broadcasted_iota(jnp.int32, (rows, LANES), 1)
    sub = lax.broadcasted_iota(jnp.int32, (rows, LANES), 0)
    for g in range(regions):
        start = starts_s[me, g]
        first = start // LANES
        rest = lax.rem(start, LANES)
        shift = lax.rem(LANES - rest, LANES)
        low = lane < LANES - rest
        left = pltpu.roll(xs[first], shift, 1)
        for b in range(blocks):
            right = pltpu.roll(xs[first + b + 1], shift, 1)
            y = jnp.where(low, left, right)
            high = y.astype(jnp.bfloat16).astype(jnp.float32)
            pair = jnp.concatenate([high, y - high], axis=0).astype(jnp.bfloat16)
            ys[g * 2 * rows:(g + 1) * 2 * rows, b * LANES:(b + 1) * LANES] = pair
            left = right

    total = None
    for k in range(chunks):
        late[k].wait()
        part = lax.dot_general(ys[:, k * CHUNK:(k + 1) * CHUNK], table_v[k], (((1,), (1,)), ((), ())),
                               preferred_element_type=jnp.float32)
        total = part if total is None else total + part

    lags = rows + 1
    pad = -(lags * cb) % LANES
    total = jnp.concatenate([total, jnp.zeros((total.shape[0], pad), jnp.float32)], axis=1)
    spot = lax.rem(me, per) * cb
    mine = (lane >= spot) & (lane < spot + cb)
    for g in range(regions):
        pg = total[g * 2 * rows:g * 2 * rows + rows] + total[g * 2 * rows + rows:(g + 1) * 2 * rows]
        lag = []
        for d in range(lags):
            tile = pg[:, d // per * LANES:(d // per + 1) * LANES]
            lag.append(pltpu.roll(tile, lax.rem(spot + LANES - d % per * cb, LANES), 1))
        own = lag[0]
        after = jnp.where(sub >= half, lag[rows], 0.0)
        before = jnp.where(sub < half, lag[rows], 0.0)
        for e in range(1, rows):
            a = pltpu.roll(lag[e], e, 0)
            b = pltpu.roll(lag[rows - e], e, 0)
            own = own + jnp.where(sub >= e, a, b)
            other = jnp.where(sub >= e, b, a)
            source = lax.rem(sub + rows - e, rows)
            after = after + jnp.where(source >= half, other, 0.0)
            before = before + jnp.where(source < half, other, 0.0)
        sbuf[0, g] = jnp.where(mine, before, 0.0).astype(jnp.bfloat16)
        sbuf[1, g] = jnp.where(mine, own, 0.0).astype(jnp.bfloat16)
        sbuf[2, g] = jnp.where(mine, after, 0.0).astype(jnp.bfloat16)

    pl.semaphore_wait(barrier, len(links))

    def message(step, delta):
        to = peer(step, delta)
        region = to["ang"]
        return pltpu.make_async_remote_copy(
            src_ref=sbuf.at[delta + 1, region], dst_ref=rbuf.at[delta + 1, me],
            send_sem=send_sem.at[delta + 1, region], recv_sem=recv_sem.at[delta + 1, me],
            device_id=to, device_id_type=pl.DeviceIdType.MESH)

    sent = [message(step, delta) for step, delta in links]
    for copy in sent:
        copy.start()
    weight_load.wait()

    def arrived(step, delta):
        angle = lax.rem(me + step, regions)
        pltpu.make_async_remote_copy(
            src_ref=sbuf.at[delta + 1, angle], dst_ref=rbuf.at[delta + 1, angle],
            send_sem=send_sem.at[delta + 1, angle], recv_sem=recv_sem.at[delta + 1, angle],
            device_id=peer(step, delta), device_id_type=pl.DeviceIdType.MESH).wait_recv()

    rbuf[1, me] = sbuf[1, me]
    for step, delta in links:
        arrived(step, delta)

    result = jnp.zeros(out.shape, jnp.float32)
    for group in range(-(-angles // per)):
        block = jnp.zeros((rows, LANES), jnp.float32)
        members = range(group * per, min(angles, (group + 1) * per))
        for a in members:
            block = block + rbuf[1, a].astype(jnp.float32)
            block = block + jnp.where(row < tiles - 1, rbuf[0, a].astype(jnp.float32), 0.0)
            block = block + jnp.where(row > 0, rbuf[2, a].astype(jnp.float32), 0.0)
        block = block.astype(jnp.bfloat16)
        depth = len(members) * cb
        w = weights_v[group * per:group * per + len(members)].reshape(depth, out.shape[1])
        result = result + jnp.dot(block[:, :depth], w, preferred_element_type=jnp.float32)
    out_v[...] = result
    store = pltpu.make_async_copy(out_v, out, out_sem)
    store.start()
    for copy in sent:
        copy.wait_send()
    store.wait()


def body(projections, flats, block_start, bp_weights):
    _, rows, width = projections.shape
    angles, cb, pixels = bp_weights.shape
    regions, tiles = lax.axis_size("ang"), lax.axis_size("row")
    table = jnp.asarray(filter_table(rows + 2 * HALO, width, cb), jnp.bfloat16)
    hbm = pl.BlockSpec(memory_space=pl.ANY)
    return pl.pallas_call(
        functools.partial(kernel, regions, tiles),
        name="fbp",
        out_shape=jax.ShapeDtypeStruct((rows, pixels), jnp.float32),
        in_specs=[hbm, hbm, hbm, hbm, hbm],
        out_specs=hbm,
        scratch_shapes=[
            pltpu.SMEM(block_start.shape, jnp.int32),
            pltpu.VMEM((rows, width), jnp.bfloat16),
            pltpu.VMEM((rows, width), jnp.float32),
            pltpu.VMEM(table.shape, jnp.bfloat16),
            pltpu.VMEM(bp_weights.shape, jnp.bfloat16),
            pltpu.VMEM((2 * width // LANES, rows, LANES), jnp.float32),
            pltpu.VMEM((regions * 2 * rows, width), jnp.bfloat16),
            pltpu.VMEM((3, regions, rows, LANES), jnp.bfloat16),
            pltpu.VMEM((3, angles, rows, LANES), jnp.bfloat16),
            pltpu.VMEM((rows, pixels), jnp.float32),
            pltpu.SemaphoreType.DMA((4,)),
            pltpu.SemaphoreType.DMA((table.shape[0],)),
            pltpu.SemaphoreType.DMA,
            pltpu.SemaphoreType.DMA((3, regions)),
            pltpu.SemaphoreType.DMA((3, angles)),
        ],
        compiler_params=pltpu.CompilerParams(collective_id=0, has_side_effects=True),
    )(block_start, projections, flats, table, bp_weights)


def solution(mesh):
    placed = (P(("scan", "ang"), "row", None), P(("scan", "row"), None), P(), P(None, None, "ang"))
    return jax.shard_map(
        body, mesh=mesh, in_specs=placed, out_specs=P(("scan", "row"), "ang"), check_vma=False
    )
```

time: 34.1 us -> 12 us (0.35)
  the two profiles are of different devices: /device:TPU:0 before, /device:TPU:1 now
where the time goes in v1:
time: 12 us; the launch traced here: 11.8 us
  Pallas kernels  10.5 us (88%)
  local copies, waits for them, and re-layouts  1.3 us (11%)
    pallas_call x1, Pallas kernels, body(): pl.pallas_call(functools.partial(kernel, regions, tiles), name='fbp', out...  10.5 us
    unnamed x1, local copies, waits for them, and re-layouts  1.3 us

profile of v1, /device:TPU:1, one launch (start us, length us, event | category | flops | bytes accessed | tf_op | source)
XLA Modules:
  0.0 11.8 jit_solution(1671992036307523284)
XLA Ops:
  0.0 10.5 %fbp.1 = f32[8,256]{1,0:T(8,128)} custom-call(s32[4,4]{1,0:T(4,128)} %starts.1, bf16[1,8,2560]{2,1,0:T(8,128)(2,1)} %proj.1, f32[8,2560]{1,0:T(8,128)} %flats.1, bf16[5,288,512]{2,1,0:T(8,128)(2,1)} %constant.2.clone.table, bf16[4,32,256]{2,1,0:T(8,128)(2,1)} %weights.1), custom_call_target="tpu_custom_call" | custom-call | tf_op jit(solution)/shard_map/fbp/pallas_call | solution.py:171
  10.5 1.3 %copy.7 = f32[8,256]{1,0:T(8,128)} copy(f32[8,256]{1,0:T(8,128)} %fbp.1) | data formatting | bytes 16384

commit v2 on v1

--- a/solution.py
+++ b/solution.py
@@ -30,8 +30,8 @@
 
 
 def kernel(regions, tiles, starts, proj, flats, table, weights, out,
-           starts_s, proj_v, flats_v, table_v, weights_v, xs, ys, sbuf, rbuf, out_v,
-           load_sem, table_sem, out_sem, send_sem, recv_sem):
+           starts_s, proj_v, flats_v, table_v, weights_v, xs, ys, sbuf, rbuf,
+           load_sem, table_sem, send_sem, recv_sem):
     rows, width = flats.shape
     blocks = width // LANES
     chunks = table.shape[0]
@@ -154,12 +154,9 @@
         depth = len(members) * cb
         w = weights_v[group * per:group * per + len(members)].reshape(depth, out.shape[1])
         result = result + jnp.dot(block[:, :depth], w, preferred_element_type=jnp.float32)
-    out_v[...] = result
-    store = pltpu.make_async_copy(out_v, out, out_sem)
-    store.start()
+    out[...] = result
     for copy in sent:
         copy.wait_send()
-    store.wait()
 
 
 def body(projections, flats, block_start, bp_weights):
@@ -167,13 +164,13 @@
     angles, cb, pixels = bp_weights.shape
     regions, tiles = lax.axis_size("ang"), lax.axis_size("row")
     table = jnp.asarray(filter_table(rows + 2 * HALO, width, cb), jnp.bfloat16)
-    hbm = pl.BlockSpec(memory_space=pl.ANY)
+    hbm = pl.BlockSpec(memory_space=pltpu.HBM)
     return pl.pallas_call(
         functools.partial(kernel, regions, tiles),
         name="fbp",
-        out_shape=jax.ShapeDtypeStruct((rows, pixels), jnp.float32),
+        out_shape=pltpu.VMEM((rows, pixels), jnp.float32),
         in_specs=[hbm, hbm, hbm, hbm, hbm],
-        out_specs=hbm,
+        out_specs=pl.BlockSpec(memory_space=pltpu.VMEM),
         scratch_shapes=[
             pltpu.SMEM(block_start.shape, jnp.int32),
             pltpu.VMEM((rows, width), jnp.bfloat16),
@@ -184,14 +181,12 @@
             pltpu.VMEM((regions * 2 * rows, width), jnp.bfloat16),
             pltpu.VMEM((3, regions, rows, LANES), jnp.bfloat16),
             pltpu.VMEM((3, angles, rows, LANES), jnp.bfloat16),
-            pltpu.VMEM((rows, pixels), jnp.float32),
             pltpu.SemaphoreType.DMA((4,)),
             pltpu.SemaphoreType.DMA((table.shape[0],)),
-            pltpu.SemaphoreType.DMA,
             pltpu.SemaphoreType.DMA((3, regions)),
             pltpu.SemaphoreType.DMA((3, angles)),
         ],
-        compiler_params=pltpu.CompilerParams(collective_id=0, has_side_effects=True),
+        compiler_params=pltpu.CompilerParams(collective_id=0, has_side_effects=True, vmem_limit_bytes=65000000),
     )(block_start, projections, flats, table, bp_weights)
 
 

time: 12 us -> 10.6 us (0.88)
  local copies, waits for them, and re-layouts: 1.3 us -> 0.6 us
  Pallas kernels: 10.5 us -> 9.88 us
    unnamed x1, local copies, waits for them, and re-layouts: 1.3 us -> 0.6 us
    pallas_call x1, Pallas kernels: 10.5 us -> 9.88 us  [body(): pl.pallas_call(functools.partial(kernel, regions, tiles), name='fbp', out...]
where the time goes in v2:
time: 10.6 us; the launch traced here: 10.5 us
  Pallas kernels  9.88 us (93%)
  local copies, waits for them, and re-layouts  0.6 us (6%)
    pallas_call x1, Pallas kernels, body(): pl.pallas_call(functools.partial(kernel, regions, tiles), name='fbp', out...  9.88 us
    unnamed x1, local copies, waits for them, and re-layouts  0.6 us

profile of v2, /device:TPU:1, one launch (start us, length us, event | category | flops | bytes accessed | tf_op | source)
XLA Modules:
  0.0 10.5 jit_solution(6906112004446216610)
XLA Ops:
  0.0 9.9 %fbp.1 = f32[8,256]{1,0:T(8,128)S(1)} custom-call(s32[4,4]{1,0:T(4,128)} %starts.1, bf16[1,8,2560]{2,1,0:T(8,128)(2,1)} %proj.1, f32[8,2560]{1,0:T(8,128)} %flats.1, bf16[5,288,512]{2,1,0:T(8,128)(2,1)} %constant.2.clone.table, bf16[4,32,256]{2,1,0:T(8,128)(2,1)} %weights.1), custom_call_target="tpu_custom_call" | custom-call | tf_op jit(solution)/shard_map/fbp/pallas_call | solution.py:168
  9.9 0.6 %copy.7 = f32[8,256]{1,0:T(8,128)} copy(f32[8,256]{1,0:T(8,128)S(1)} %fbp.1) | data formatting | bytes 16384

commit v3 on v2

--- a/solution.py
+++ b/solution.py
@@ -11,6 +11,7 @@
 HALO = 4
 LANES = 128
 CHUNK = 512
+SHIFTS = 2
 paganin_beta = 8.0
 ramp_gain = 320.0
 
@@ -23,6 +24,7 @@
     ramp = ramp_gain * (folded / width) * (0.5 + 0.5 * np.cos(2.0 * np.pi * folded / width))
     taps = np.real(np.fft.ifft2(ramp[None, :] / (1.0 + paganin_beta * lam)))
     lags = tile_rows // 2 + 1
+    cb_width = cb_width // SHIFTS
     place = (np.arange(cb_width)[:, None] - np.arange(width)[None, :]) % width
     table = taps[:lags][:, place].reshape(lags * cb_width, width)
     chunks = width // CHUNK
@@ -45,9 +47,12 @@
         return {"ang": lax.rem(me + step, regions), "row": lax.rem(row + delta + tiles, tiles)}
 
     links = [(step, delta) for step in range(regions) for delta in (-1, 0, 1) if (step, delta) != (0, 0)]
-    barrier = pltpu.get_barrier_semaphore()
-    for step, delta in links:
-        pl.semaphore_signal(barrier, inc=1, device_id=peer(step, delta), device_id_type=pl.DeviceIdType.MESH)
+
+    def when_there(delta, action):
+        if delta == 0:
+            action()
+        else:
+            pl.when(row > 0 if delta < 0 else row < tiles - 1)(action)
 
     loads = [pltpu.make_async_copy(proj.at[0], proj_v, load_sem.at[0]),
              pltpu.make_async_copy(flats, flats_v, load_sem.at[1]),
@@ -56,6 +61,15 @@
     weight_load = pltpu.make_async_copy(weights, weights_v, load_sem.at[2])
     for copy in loads + late + [weight_load]:
         copy.start()
+
+    barrier = pltpu.get_barrier_semaphore()
+    for step, delta in links:
+        when_there(delta, lambda: pl.semaphore_signal(
+            barrier, inc=1, device_id=peer(step, delta), device_id_type=pl.DeviceIdType.MESH))
+    zeros = jnp.zeros((angles, rows, LANES), jnp.bfloat16)
+    pl.when(row == tiles - 1)(lambda: rbuf.at[0].__setitem__(..., zeros))
+    pl.when(row == 0)(lambda: rbuf.at[2].__setitem__(..., zeros))
+
     for copy in loads:
         copy.wait()
 
@@ -68,20 +82,20 @@
 
     lane = lax.broadcasted_iota(jnp.int32, (rows, LANES), 1)
     sub = lax.broadcasted_iota(jnp.int32, (rows, LANES), 0)
+    cs = cb // SHIFTS
     for g in range(regions):
-        start = starts_s[me, g]
-        first = start // LANES
-        rest = lax.rem(start, LANES)
-        shift = lax.rem(LANES - rest, LANES)
-        low = lane < LANES - rest
-        left = pltpu.roll(xs[first], shift, 1)
+        shifted = []
+        for k in range(SHIFTS):
+            start = starts_s[me, g] + k * cs
+            first = start // LANES
+            rest = lax.rem(start, LANES)
+            shift = lax.rem(LANES - rest, LANES)
+            low = lane < LANES - rest
+            turned = [pltpu.roll(xs[first + b], shift, 1) for b in range(blocks + 1)]
+            shifted.append([jnp.where(low, turned[b], turned[b + 1]) for b in range(blocks)])
         for b in range(blocks):
-            right = pltpu.roll(xs[first + b + 1], shift, 1)
-            y = jnp.where(low, left, right)
-            high = y.astype(jnp.bfloat16).astype(jnp.float32)
-            pair = jnp.concatenate([high, y - high], axis=0).astype(jnp.bfloat16)
-            ys[g * 2 * rows:(g + 1) * 2 * rows, b * LANES:(b + 1) * LANES] = pair
-            left = right
+            ys[g * SHIFTS * rows:(g + 1) * SHIFTS * rows, b * LANES:(b + 1) * LANES] = jnp.concatenate(
+                [y[b] for y in shifted], axis=0).astype(jnp.bfloat16)
 
     total = None
     for k in range(chunks):
@@ -91,16 +105,21 @@
         total = part if total is None else total + part
 
     lags = rows + 1
-    pad = -(lags * cb) % LANES
+    pad = -(lags * cs) % LANES
     total = jnp.concatenate([total, jnp.zeros((total.shape[0], pad), jnp.float32)], axis=1)
     spot = lax.rem(me, per) * cb
     mine = (lane >= spot) & (lane < spot + cb)
     for g in range(regions):
-        pg = total[g * 2 * rows:g * 2 * rows + rows] + total[g * 2 * rows + rows:(g + 1) * 2 * rows]
         lag = []
         for d in range(lags):
-            tile = pg[:, d // per * LANES:(d // per + 1) * LANES]
-            lag.append(pltpu.roll(tile, lax.rem(spot + LANES - d % per * cb, LANES), 1))
+            column = d * cs // LANES * LANES
+            merged = None
+            for k in range(SHIFTS):
+                base = (g * SHIFTS + k) * rows
+                tile = total[base:base + rows, column:column + LANES]
+                tile = pltpu.roll(tile, lax.rem(spot + k * cs + LANES - d * cs % LANES, LANES), 1)
+                merged = tile if k == 0 else jnp.where(lane < spot + k * cs, merged, tile)
+            lag.append(merged)
         own = lag[0]
         after = jnp.where(sub >= half, lag[rows], 0.0)
         before = jnp.where(sub < half, lag[rows], 0.0)
@@ -116,7 +135,8 @@
         sbuf[1, g] = jnp.where(mine, own, 0.0).astype(jnp.bfloat16)
         sbuf[2, g] = jnp.where(mine, after, 0.0).astype(jnp.bfloat16)
 
-    pl.semaphore_wait(barrier, len(links))
+    sides = (row > 0).astype(jnp.int32) + (row < tiles - 1).astype(jnp.int32)
+    pl.semaphore_wait(barrier, regions - 1 + sides * regions)
 
     def message(step, delta):
         to = peer(step, delta)
@@ -127,16 +147,17 @@
             device_id=to, device_id_type=pl.DeviceIdType.MESH)
 
     sent = [message(step, delta) for step, delta in links]
-    for copy in sent:
-        copy.start()
+    for (step, delta), copy in zip(links, sent):
+        when_there(delta, copy.start)
     weight_load.wait()
 
     def arrived(step, delta):
         angle = lax.rem(me + step, regions)
-        pltpu.make_async_remote_copy(
+        copy = pltpu.make_async_remote_copy(
             src_ref=sbuf.at[delta + 1, angle], dst_ref=rbuf.at[delta + 1, angle],
             send_sem=send_sem.at[delta + 1, angle], recv_sem=recv_sem.at[delta + 1, angle],
-            device_id=peer(step, delta), device_id_type=pl.DeviceIdType.MESH).wait_recv()
+            device_id=peer(step, delta), device_id_type=pl.DeviceIdType.MESH)
+        when_there(-delta, copy.wait_recv)
 
     rbuf[1, me] = sbuf[1, me]
     for step, delta in links:
@@ -148,15 +169,15 @@
         members = range(group * per, min(angles, (group + 1) * per))
         for a in members:
             block = block + rbuf[1, a].astype(jnp.float32)
-            block = block + jnp.where(row < tiles - 1, rbuf[0, a].astype(jnp.float32), 0.0)
-            block = block + jnp.where(row > 0, rbuf[2, a].astype(jnp.float32), 0.0)
+            block = block + rbuf[0, a].astype(jnp.float32)
+            block = block + rbuf[2, a].astype(jnp.float32)
         block = block.astype(jnp.bfloat16)
         depth = len(members) * cb
         w = weights_v[group * per:group * per + len(members)].reshape(depth, out.shape[1])
         result = result + jnp.dot(block[:, :depth], w, preferred_element_type=jnp.float32)
     out[...] = result
-    for copy in sent:
-        copy.wait_send()
+    for (step, delta), copy in zip(links, sent):
+        when_there(delta, copy.wait_send)
 
 
 def body(projections, flats, block_start, bp_weights):
@@ -178,7 +199,7 @@
             pltpu.VMEM(table.shape, jnp.bfloat16),
             pltpu.VMEM(bp_weights.shape, jnp.bfloat16),
             pltpu.VMEM((2 * width // LANES, rows, LANES), jnp.float32),
-            pltpu.VMEM((regions * 2 * rows, width), jnp.bfloat16),
+            pltpu.VMEM((regions * SHIFTS * rows, width), jnp.bfloat16),
             pltpu.VMEM((3, regions, rows, LANES), jnp.bfloat16),
             pltpu.VMEM((3, angles, rows, LANES), jnp.bfloat16),
             pltpu.SemaphoreType.DMA((4,)),

time: 10.6 us -> 10.3 us (0.972)
  Pallas kernels: 9.88 us -> 9.5 us
    pallas_call x1, Pallas kernels: 9.88 us -> 9.5 us  [body(): pl.pallas_call(functools.partial(kernel, regions, tiles), name='fbp', out...]
where the time goes in v3:
time: 10.3 us; the launch traced here: 10.1 us
  Pallas kernels  9.5 us (92%)
  local copies, waits for them, and re-layouts  0.6 us (6%)
    pallas_call x1, Pallas kernels, body(): pl.pallas_call(functools.partial(kernel, regions, tiles), name='fbp', out...  9.5 us
    unnamed x1, local copies, waits for them, and re-layouts  0.6 us

profile of v3, /device:TPU:1, one launch (start us, length us, event | category | flops | bytes accessed | tf_op | source)
XLA Modules:
  0.0 10.1 jit_solution(16552251568012061133)
XLA Ops:
  0.0 9.5 %fbp.1 = f32[8,256]{1,0:T(8,128)S(1)} custom-call(s32[4,4]{1,0:T(4,128)} %starts.1, bf16[1,8,2560]{2,1,0:T(8,128)(2,1)} %proj.1, f32[8,2560]{1,0:T(8,128)} %flats.1, bf16[5,144,512]{2,1,0:T(8,128)(2,1)} %constant.2.clone.table, bf16[4,32,256]{2,1,0:T(8,128)(2,1)} %weights.1), custom_call_target="tpu_custom_call" | custom-call | tf_op jit(solution)/shard_map/fbp/pallas_call | solution.py:189
  9.5 0.6 %copy.7 = f32[8,256]{1,0:T(8,128)} copy(f32[8,256]{1,0:T(8,128)S(1)} %fbp.1) | data formatting | bytes 16384

commit v4 on v3

--- a/solution.py
+++ b/solution.py
@@ -10,7 +10,6 @@
 
 HALO = 4
 LANES = 128
-CHUNK = 512
 SHIFTS = 2
 paganin_beta = 8.0
 ramp_gain = 320.0
@@ -26,9 +25,7 @@
     lags = tile_rows // 2 + 1
     cb_width = cb_width // SHIFTS
     place = (np.arange(cb_width)[:, None] - np.arange(width)[None, :]) % width
-    table = taps[:lags][:, place].reshape(lags * cb_width, width)
-    chunks = width // CHUNK
-    return table.reshape(lags * cb_width, chunks, CHUNK).transpose(1, 0, 2)
+    return taps[:lags][:, place].reshape(lags * cb_width, width)
 
 
 def kernel(regions, tiles, starts, proj, flats, table, weights, out,
@@ -36,7 +33,6 @@
            load_sem, table_sem, send_sem, recv_sem):
     rows, width = flats.shape
     blocks = width // LANES
-    chunks = table.shape[0]
     angles, cb, _ = weights.shape
     per = LANES // cb
     half = rows // 2
@@ -57,7 +53,7 @@
     loads = [pltpu.make_async_copy(proj.at[0], proj_v, load_sem.at[0]),
              pltpu.make_async_copy(flats, flats_v, load_sem.at[1]),
              pltpu.make_async_copy(starts, starts_s, load_sem.at[3])]
-    late = [pltpu.make_async_copy(table.at[k], table_v.at[k], table_sem.at[k]) for k in range(chunks)]
+    late = [pltpu.make_async_copy(table, table_v, table_sem)]
     weight_load = pltpu.make_async_copy(weights, weights_v, load_sem.at[2])
     for copy in loads + late + [weight_load]:
         copy.start()
@@ -97,12 +93,8 @@
             ys[g * SHIFTS * rows:(g + 1) * SHIFTS * rows, b * LANES:(b + 1) * LANES] = jnp.concatenate(
                 [y[b] for y in shifted], axis=0).astype(jnp.bfloat16)
 
-    total = None
-    for k in range(chunks):
-        late[k].wait()
-        part = lax.dot_general(ys[:, k * CHUNK:(k + 1) * CHUNK], table_v[k], (((1,), (1,)), ((), ())),
-                               preferred_element_type=jnp.float32)
-        total = part if total is None else total + part
+    late[0].wait()
+    total = lax.dot_general(ys[...], table_v[...], (((1,), (1,)), ((), ())), preferred_element_type=jnp.float32)
 
     lags = rows + 1
     pad = -(lags * cs) % LANES
@@ -203,7 +195,7 @@
             pltpu.VMEM((3, regions, rows, LANES), jnp.bfloat16),
             pltpu.VMEM((3, angles, rows, LANES), jnp.bfloat16),
             pltpu.SemaphoreType.DMA((4,)),
-            pltpu.SemaphoreType.DMA((table.shape[0],)),
+            pltpu.SemaphoreType.DMA,
             pltpu.SemaphoreType.DMA((3, regions)),
             pltpu.SemaphoreType.DMA((3, angles)),
         ],

time: 10.3 us -> 9.79 us (0.950)
  Pallas kernels: 9.5 us -> 9.04 us
    pallas_call x1, Pallas kernels: 9.5 us -> 9.04 us  [body(): pl.pallas_call(functools.partial(kernel, regions, tiles), name='fbp', out...]
where the time goes in v4:
time: 9.79 us; the launch traced here: 9.65 us
  Pallas kernels  9.04 us (92%)
  local copies, waits for them, and re-layouts  0.6 us (6%)
    pallas_call x1, Pallas kernels, body(): pl.pallas_call(functools.partial(kernel, regions, tiles), name='fbp', out...  9.04 us
    unnamed x1, local copies, waits for them, and re-layouts  0.6 us

profile of v4, /device:TPU:1, one launch (start us, length us, event | category | flops | bytes accessed | tf_op | source)
XLA Modules:
  0.0 9.6 jit_solution(5316032810069169426)
XLA Ops:
  0.0 9.0 %fbp.1 = f32[8,256]{1,0:T(8,128)S(1)} custom-call(s32[4,4]{1,0:T(4,128)} %starts.1, bf16[1,8,2560]{2,1,0:T(8,128)(2,1)} %proj.1, f32[8,2560]{1,0:T(8,128)} %flats.1, bf16[144,2560]{1,0:T(8,128)(2,1)} %constant.2.clone.table, bf16[4,32,256]{2,1,0:T(8,128)(2,1)} %weights.1), custom_call_target="tpu_custom_call" | custom-call | tf_op jit(solution)/shard_map/fbp/pallas_call | solution.py:181
  9.0 0.6 %copy.7 = f32[8,256]{1,0:T(8,128)} copy(f32[8,256]{1,0:T(8,128)S(1)} %fbp.1) | data formatting | bytes 16384
